TPU v7x, 32 devices: a whole 2x2x4 slice. The times are simulated.
32 devices in a mesh: tp: 8 (over z, y), rep: 4 (over x, core).
Axes of the slice: x: 2, y: 2, z: 4, core: 2. Of those that a mesh axis runs over, the one named last changes fastest.
Arguments:
- tokens: bfloat16 [1536, 8192], P('rep', 'tp'), may hold values from -6 to 6
- row_lengths: int32 [8], P('rep'), may hold values from 1 to 192
- attn_gain: float32 [8192], P('tp'), may hold values from 0.1 to 1.9
- query_weight: bfloat16 [8192, 4096], P('rep', 'tp'), may hold values from -2 to 2
- key_weight: bfloat16 [8192, 512], P('rep', 'tp'), may hold values from -2 to 2
- value_matrix: bfloat16 [8192, 512], P('rep', 'tp'), may hold values from -0.0625 to 0.0625
- output_weight: bfloat16 [4096, 8192], P('rep', 'tp'), may hold values from -0.09375 to 0.09375
- final_gain: float32 [8192], P('tp'), may hold values from 0.1 to 1.9
- value_head: float32 [8192, 6], P('tp'), may hold values from -0.0625 to 0.0625
Outputs:
- resid_out: bfloat16 [1536, 8192], P('rep', 'tp')
- objective_scores: float32 [1536, 6], P('rep')
All inputs are finite; a program needn't handle non-finite values.
Results may differ from a plain program's by a relative error of at most 0.025.
Values may be sent and summed in bfloat16 or wider, within the bound.
A program may use at most 64 MiB of HBM per device.

v0:
```python
import jax
import jax.numpy as jnp
from jax import lax
from jax.sharding import PartitionSpec as P

KEY_VALUE_HEADS = 4
HEAD_SIZE = 128
EPS = 1e-05


def local(
    tokens,
    row_lengths,
    attn_gain,
    query_weight,
    key_weight,
    value_matrix,
    output_weight,
    final_gain,
    value_head,
):
    width = tokens.shape[1] * lax.axis_size("tp")
    xfloat = tokens.astype(jnp.float32)
    total = lax.psum(jnp.sum(xfloat * xfloat, axis=1), "tp")
    first_scale = lax.rsqrt(total / width + EPS)[:, None]
    normed = lax.all_gather(
        (xfloat * first_scale * attn_gain).astype(jnp.bfloat16), "tp", axis=1, tiled=True
    )
    rows_here = normed.shape[0]
    head_cols = query_weight.shape[1]
    pieces = (
        lax.all_gather(query_weight, "rep", axis=0, tiled=True),
        lax.all_gather(key_weight, "rep", axis=0, tiled=True),
        lax.all_gather(value_matrix, "rep", axis=0, tiled=True),
    )
    columns = normed
    query, key_rows, value_rows = tuple(
        (jnp.dot(columns, piece, preferred_element_type=jnp.float32) for piece in pieces)
    )
    query = query.astype(jnp.bfloat16)
    key_rows = key_rows.astype(jnp.bfloat16)
    value_rows = value_rows.astype(jnp.bfloat16)
    key_full, value_full = (
        lax.all_gather(key_rows, "tp", axis=1, tiled=True),
        lax.all_gather(value_rows, "tp", axis=1, tiled=True),
    )
    local_heads = head_cols // HEAD_SIZE
    sequence_rows = row_lengths.shape[0]
    row_length_count = rows_here // sequence_rows
    first_head = lax.axis_index("tp") * local_heads
    key_value_index = (first_head + jnp.arange(local_heads, dtype=jnp.int32)) % KEY_VALUE_HEADS
    query4 = query.reshape(sequence_rows, row_length_count, local_heads, HEAD_SIZE)
    key_tensor4 = jnp.take(
        key_full.reshape(sequence_rows, row_length_count, KEY_VALUE_HEADS, HEAD_SIZE),
        key_value_index,
        axis=2,
    )
    value_tensor4 = jnp.take(
        value_full.reshape(sequence_rows, row_length_count, KEY_VALUE_HEADS, HEAD_SIZE),
        key_value_index,
        axis=2,
    )
    scores = jnp.einsum(
        "rqhd,rkhd->rhqk", query4, key_tensor4, preferred_element_type=jnp.float32
    ) * (1.0 / HEAD_SIZE**0.5)
    position = jnp.arange(row_length_count, dtype=jnp.int32)
    causal = position[None, :] <= position[:, None]
    allowed = causal[None, None, :, :] & (
        position[None, None, None, :] < row_lengths[:, None, None, None]
    )
    scores = jnp.where(allowed, scores, jnp.float32(-1e30))
    scores = scores - jnp.max(scores, axis=3, keepdims=True)
    expo = jnp.exp(scores)
    probs = (expo / jnp.sum(expo, axis=3, keepdims=True)).astype(jnp.bfloat16)
    attended = jnp.einsum(
        "rhqk,rkhd->rqhd", probs, value_tensor4, preferred_element_type=jnp.float32
    )
    attended = attended.astype(jnp.bfloat16).reshape(rows_here, head_cols)
    mixed_all = lax.all_gather(attended, "tp", axis=1, tiled=True)
    columns = mixed_all
    update = jnp.dot(
        columns,
        lax.all_gather(output_weight, "rep", axis=0, tiled=True),
        preferred_element_type=jnp.float32,
    )
    resid_out = (xfloat + update).astype(jnp.bfloat16)
    rfloat = resid_out.astype(jnp.float32)
    squares = jnp.sum(rfloat * rfloat, axis=1)
    local_scores = jnp.dot(rfloat * final_gain, value_head, precision=lax.Precision.HIGHEST)
    total_out, weighted = lax.psum((squares, local_scores), "tp")
    logits = weighted * lax.rsqrt(total_out / width + EPS)[:, None]
    live = (position[None, :] < row_lengths[:, None]).reshape(rows_here, 1)
    objective_scores = jnp.where(live, logits, jnp.float32(0.0))
    return (resid_out, objective_scores)


def solution(mesh):
    in_specs = (
        P("rep", "tp"),
        P("rep"),
        P("tp"),
        P("rep", "tp"),
        P("rep", "tp"),
        P("rep", "tp"),
        P("rep", "tp"),
        P("tp"),
        P("tp", None),
    )
    out_specs = (P("rep", "tp"), P("rep", None))
    return jax.shard_map(local, mesh=mesh, in_specs=in_specs, out_specs=out_specs, check_vma=False)
```

profile of v0, /device:TPU:0, one launch (start us, length us, event | category | flops | bytes accessed | tf_op | source)
XLA Modules:
  0.0 382.7 jit_solution(16926781889026036177)
XLA Ops:
  7.2 0.0 copy-start
  7.2 0.0 copy-start.1
  7.2 0.0 all-gather.9.cloned.1.call-start
  7.2 0.7 all-gather.9.cloned.1.call-update
  7.9 0.0 all-gather.7.cloned.1.call-start
  8.0 1.4 fusion.4
  9.3 23.1 %psum.21 = f32[384]{0:T(512)S(1)} all-reduce(f32[384]{0:T(512)S(1)} %fusion.4), channel_id=1, replica_groups=mesh['tp'=8,'rep'=4] {'tp'}, use_global_device_ids=true, to_apply=%region_1.0 | all-reduce | flops 384 | bytes 3072 | tf_op jit(solution)/shard_map/psum | solution.py:24
  32.5 0.0 copy-done.1
  32.5 1.8 fusion.6
  34.3 0.0 all-gather.7.cloned.1.call-update
  34.3 0.0 all-gather.13.cloned.1.call-start
  34.4 0.7 all-gather.13.cloned.1.call-update
  35.1 0.0 all-gather.11.cloned.1.call-start
  35.1 0.5 all-gather.11.cloned.1.call-update
  35.7 0.0 copy-start.4
  35.7 0.0 all-gather.17.cloned.1.call-start
  35.7 0.5 all-gather.17.cloned.1.call-update
  36.3 0.0 all-gather.15.cloned.1.call-start
  36.4 0.0 copy-done.4
  36.4 0.1 iota_compare_fusion.1
  36.5 0.1 broadcast_and_fusion
  36.6 0.0 all-gather.9.cloned.1.call-done
  36.6 93.9 %all-gather.7.cloned.1.call-done = bf16[384,8192]{1,0:T(8,128)(2,1)} async-done(((bf16[384,1024]{1,0:T(8,128)(2,1)}), bf16[384,8192]{1,0:T(8,128)(2,1)}) %all-gather.7.cloned.1.call-update) | async-done | bytes 6291472 | tf_op jit(solution)/shard_map/all_gather | solution.py:26
  130.5 5.1 %convolution_convert_fusion.3 = bf16[384,64]{0,1:T(8,128)(2,1)S(1)} fusion(bf16[384,8192]{1,0:T(8,128)(2,1)} %all-gather.7.cloned.1.call-done, bf16[8192,64]{0,1:T(8,128)(2,1)} %all-gather.9.cloned.1.call-done), kind=kOutput, calls=%fused_computation.22 | convolution fusion | flops 402677760 | bytes 7389184 | tf_op jit(solution)/shard_map/dot_general | solution.py:38
  135.6 31.0 %all_gather.26 = bf16[384,512]{0,1:T(8,128)(2,1)S(1)} all-gather(bf16[384,64]{0,1:T(8,128)(2,1)S(1)} %convolution_convert_fusion.3), channel_id=1, replica_groups=mesh['tp'=8,'rep'=4] {'tp'}, dimensions={1}, use_global_device_ids=true | all-gather | bytes 442368 | tf_op jit(solution)/shard_map/all_gather | solution.py:45
  166.6 0.3 reshape.108
  166.8 0.4 copy.14
  167.3 0.0 all-gather.13.cloned.1.call-done
  167.3 5.1 %convolution_convert_fusion.2 = bf16[384,64]{0,1:T(8,128)(2,1)S(1)} fusion(bf16[384,8192]{1,0:T(8,128)(2,1)} %all-gather.7.cloned.1.call-done, bf16[8192,64]{0,1:T(8,128)(2,1)} %all-gather.13.cloned.1.call-done), kind=kOutput, calls=%fused_computation.21 | convolution fusion | flops 402677760 | bytes 7389184 | tf_op jit(solution)/shard_map/dot_general | solution.py:38
  172.4 31.1 %all_gather.29 = bf16[384,512]{0,1:T(8,128)(2,1)S(1)} all-gather(bf16[384,64]{0,1:T(8,128)(2,1)S(1)} %convolution_convert_fusion.2), channel_id=1, replica_groups=mesh['tp'=8,'rep'=4] {'tp'}, dimensions={1}, use_global_device_ids=true | all-gather | bytes 442368 | tf_op jit(solution)/shard_map/all_gather | solution.py:44
  203.6 0.3 reshape.109
  203.8 0.4 copy.16
  204.3 0.6 gather_fusion
  204.9 0.6 gather_fusion.1
  205.6 0.1 select_bitcast_fusion.1
  205.7 1.0 all-gather.11.cloned.1.call-done
  206.7 8.6 %convolution_convert_fusion.1 = bf16[384,512]{1,0:T(8,128)(2,1)S(1)} fusion(bf16[384,8192]{1,0:T(8,128)(2,1)} %all-gather.7.cloned.1.call-done, bf16[8192,512]{1,0:T(8,128)(2,1)} %all-gather.11.cloned.1.call-done), kind=kOutput, calls=%fused_computation.19 | convolution fusion | flops 3221422080 | bytes 15073280 | tf_op jit(solution)/shard_map/dot_general | solution.py:38
  215.3 0.1 reshape.83
  215.4 1.9 fusion.26
  217.3 2.0 fusion.9
  219.3 0.3 copy.21
  219.6 0.8 copy.47
  220.4 0.0 all-gather.15.cloned.1.call-update
  220.5 0.1 lt.45
  220.5 0.0 copy-start.3
  220.5 45.9 %all-gather.17.cloned.1.call-done = bf16[4096,1024]{1,0:T(8,128)(2,1)} async-done(((bf16[1024,1024]{1,0:T(8,128)(2,1)}), bf16[4096,1024]{1,0:T(8,128)(2,1)}) %all-gather.17.cloned.1.call-update) | async-done | bytes 8388624 | tf_op jit(solution)/shard_map/all_gather | solution.py:83
  266.4 65.2 %all-gather.15.cloned.1.call-done = bf16[384,4096]{1,0:T(8,128)(2,1)} async-done(((bf16[384,512]{1,0:T(8,128)(2,1)}), bf16[384,4096]{1,0:T(8,128)(2,1)}) %all-gather.15.cloned.1.call-update) | async-done | bytes 3145744 | tf_op jit(solution)/shard_map/all_gather | solution.py:79
  331.6 7.9 %fusion.3 = (f32[384]{0:T(512)S(1)}, bf16[384,1024]{1,0:T(8,128)(2,1)S(1)}) fusion(bf16[384,4096]{1,0:T(8,128)(2,1)} %all-gather.15.cloned.1.call-done, bf16[4096,1024]{1,0:T(8,128)(2,1)} %all-gather.17.cloned.1.call-done, bf16[384,1024]{1,0:T(8,128)(2,1)S(1)} %copy-done.1), kind=kOutput, calls=%fused_computation.10 | convolution fusion | flops 3223584256 | bytes 13108736 | tf_op jit(solution)/shard_map/dot_general | solution.py:81
  339.4 0.0 copy-start.2
  339.4 0.0 copy-done
  339.4 0.0 copy-done.3
  339.4 1.5 fusion.2
  340.9 34.3 %all-reduce = (f32[384,6]{0,1:T(8,128)S(1)}, f32[384]{0:T(512)S(1)}) all-reduce(f32[384,6]{0,1:T(8,128)S(1)} %fusion.2, f32[384]{0:T(512)S(1)} %get-tuple-element.9), channel_id=1, replica_groups=mesh['tp'=8,'rep'=4] {'tp'}, use_global_device_ids=true, to_apply=%region_4.6 | all-reduce | flops 2688 | bytes 21504 | tf_op jit(solution)/shard_map/psum | solution.py:90
  375.2 0.6 multiply_select_fusion.1
  375.8 0.0 copy-done.2
  (6 shorter events, 0.1 us)
Async XLA Ops:
  7.2 332.3 %copy-start = (f32[1024,6]{0,1:T(8,128)S(1)}, f32[1024,6]{0,1:T(8,128)}, u32[]{:S(2)}) copy-start(f32[1024,6]{0,1:T(8,128)} %param.19) | copy-start | bytes 73732
  7.2 25.3 %copy-start.1 = (bf16[384,1024]{1,0:T(8,128)(2,1)S(1)}, bf16[384,1024]{1,0:T(8,128)(2,1)}, u32[]{:S(2)}) copy-start(bf16[384,1024]{1,0:T(8,128)(2,1)} %param.11) | copy-start | bytes 2359300
  7.2 29.4 %all-gather.9.cloned.1.call-start = ((), (), s32[]{:S(2)}) async-start(), calls=%async_computation.1 | async-start | bytes 1310720 | tf_op jit(solution)/shard_map/all_gather | solution.py:34
  7.9 122.6 %all-gather.7.cloned.1.call-start = ((), (), s32[]{:S(2)}) async-start(), calls=%async_computation | async-start | bytes 7077888 | tf_op jit(solution)/shard_map/all_gather | solution.py:26
  34.3 133.0 %all-gather.13.cloned.1.call-start = ((), (), s32[]{:S(2)}) async-start(), calls=%async_computation.3 | async-start | bytes 1310720 | tf_op jit(solution)/shard_map/all_gather | solution.py:33
  35.1 171.6 %all-gather.11.cloned.1.call-start = ((), (), s32[]{:S(2)}) async-start(), calls=%async_computation.2 | async-start | bytes 10485760 | tf_op jit(solution)/shard_map/all_gather | solution.py:32
  35.7 0.7 copy-start.4
  35.7 230.7 %all-gather.17.cloned.1.call-start = ((), (), s32[]{:S(2)}) async-start(), calls=%async_computation.5 | async-start | bytes 10485760 | tf_op jit(solution)/shard_map/all_gather | solution.py:83
  36.3 295.3 %all-gather.15.cloned.1.call-start = ((), (), s32[]{:S(2)}) async-start(), calls=%async_computation.4 | async-start | bytes 3538944 | tf_op jit(solution)/shard_map/all_gather | solution.py:79
  220.5 118.9 %copy-start.3 = (f32[1024]{0:T(1024)S(1)}, f32[1024]{0:T(1024)}, u32[]{:S(2)}) copy-start(f32[1024]{0:T(1024)} %param.18) | copy-start | bytes 12292
  339.4 36.4 %copy-start.2 = (bf16[384,1024]{1,0:T(8,128)(2,1)}, bf16[384,1024]{1,0:T(8,128)(2,1)S(1)}, u32[]{:S(2)}) copy-start(bf16[384,1024]{1,0:T(8,128)(2,1)S(1)} %get-tuple-element.10) | copy-start | bytes 2359300
Sparse Core Ops, SparseCore 0:
  9.6 19.4 all-gather.8
  34.5 95.9 all-gather.6
  132.1 14.8 all-gather.12
  148.4 58.2 all-gather.10
  208.1 58.2 all-gather.16
  268.9 62.6 all-gather.14
where the time goes:
time: 383 us
  waiting for transfers between devices  208 us (54%)
  blocking collectives  120 us (31%)
  matrix products  32 us (8%)
  between operations  14.3 us (4%)
  other arithmetic  4.2 us (1%)
  local copies, waits for them, and re-layouts  4.01 us (1%)
    all_gather x1, waiting for transfers between devices, local(): lax.all_gather((xfloat * first_scale * attn_gain).astype(jnp.bfloat16), '...  93.9 us
    all_gather x1, waiting for transfers between devices, local(): mixed_all = lax.all_gather(attended, 'tp', axis=1, tiled=True)  65.2 us
    all_gather x1, waiting for transfers between devices, local(): lax.all_gather(output_weight, 'rep', axis=0, tiled=True)  45.9 us
    psum x1, blocking collectives, local(): total_out, weighted = lax.psum((squares, local_scores), 'tp')  34.3 us
    all_gather x1, blocking collectives, local(): lax.all_gather(key_rows, 'tp', axis=1, tiled=True)  31.1 us
    all_gather x1, blocking collectives, local(): lax.all_gather(value_rows, 'tp', axis=1, tiled=True)  31 us
    psum x1, blocking collectives, local(): total = lax.psum(jnp.sum(xfloat * xfloat, axis=1), 'tp')  23.1 us
    dot_general x3, matrix products, local(): jnp.dot(columns, piece, preferred_element_type=jnp.float32)  18.8 us
  transfers between devices with their start and end apart: 6, of which 4 were waited for; matrix products, arithmetic and copies ran while one was open for 8% of the time, Pallas kernels for 0%

commit v1 on v0

--- a/solution.py
+++ b/solution.py
@@ -76,7 +76,12 @@
         "rhqk,rkhd->rqhd", probs, value_tensor4, preferred_element_type=jnp.float32
     )
     attended = attended.astype(jnp.bfloat16).reshape(rows_here, head_cols)
-    mixed_all = lax.all_gather(attended, "tp", axis=1, tiled=True)
+    ring = [attended]
+    for hop in range(7):
+        ring.append(lax.ppermute(ring[-1], "tp", [(dev, (dev + 1) % 8) for dev in range(8)]))
+    mixed_all = jnp.roll(
+        jnp.concatenate(ring[::-1], axis=1), (lax.axis_index("tp") + 1) * ring[0].shape[1], axis=1
+    )
     columns = mixed_all
     update = jnp.dot(
         columns,

time: 383 us -> 367 us (0.958)
  waiting for transfers between devices: 208 us -> 179 us
  local copies, waits for them, and re-layouts: 4.01 us -> 20.3 us
    ppermute x0 -> x7, waiting for transfers between devices: none -> 81.1 us  [local(): lax.ppermute(ring[-1], 'tp', [(dev, (dev + 1) % 8) for dev in range(8)])]
    all_gather x1 -> x0, waiting for transfers between devices: 65.2 us -> none  [local(): mixed_all = lax.all_gather(attended, 'tp', axis=1, tiled=True)]
    all_gather x1, waiting for transfers between devices: 45.9 us -> 0.01 us  [local(): lax.all_gather(output_weight, 'rep', axis=0, tiled=True)]
    unnamed x11 -> x26, local copies, waits for them, and re-layouts: 0.83 us -> 16.4 us
  transfers between devices with their start and end apart: 6 -> 12, of which waited for: 4 -> 9; matrix products, arithmetic and copies ran while one was open for 8% -> 12% of each run, Pallas kernels for 0% -> 0%
where the time goes in v1:
time: 367 us
  waiting for transfers between devices  179 us (49%)
  blocking collectives  118 us (32%)
  matrix products  29.3 us (8%)
  local copies, waits for them, and re-layouts  20.3 us (6%)
  between operations  14 us (4%)
  other arithmetic  4.65 us (1%)
    all_gather x1, waiting for transfers between devices, local(): lax.all_gather((xfloat * first_scale * attn_gain).astype(jnp.bfloat16), '...  93.9 us
    ppermute x7, waiting for transfers between devices, local(): lax.ppermute(ring[-1], 'tp', [(dev, (dev + 1) % 8) for dev in range(8)])  81.1 us
    psum x1, blocking collectives, local(): total_out, weighted = lax.psum((squares, local_scores), 'tp')  33 us
    all_gather x1, blocking collectives, local(): lax.all_gather(value_rows, 'tp', axis=1, tiled=True)  31 us
    all_gather x1, blocking collectives, local(): lax.all_gather(key_rows, 'tp', axis=1, tiled=True)  31 us
    psum x1, blocking collectives, local(): total = lax.psum(jnp.sum(xfloat * xfloat, axis=1), 'tp')  23.1 us
    dot_general x3, matrix products, local(): jnp.dot(columns, piece, preferred_element_type=jnp.float32)  18.8 us
    unnamed x26, local copies, waits for them, and re-layouts  16.4 us
  transfers between devices with their start and end apart: 12, of which 9 were waited for; matrix products, arithmetic and copies ran while one was open for 12% of the time, Pallas kernels for 0%

profile of v1, /device:TPU:0, one launch (start us, length us, event | category | flops | bytes accessed | tf_op | source)
XLA Modules:
  0.0 366.8 jit_solution(5129945124729496308)
XLA Ops:
  7.2 0.0 all-gather.8.cloned.1.call-start
  7.2 0.7 all-gather.8.cloned.1.call-update
  7.9 0.0 all-gather.6.cloned.1.call-start
  8.0 1.4 fusion.6
  9.3 23.1 %psum.21 = f32[384]{0:T(512)S(1)} all-reduce(f32[384]{0:T(512)S(1)} %fusion.6), channel_id=1, replica_groups=mesh['tp'=8,'rep'=4] {'tp'}, use_global_device_ids=true, to_apply=%region_1.0 | all-reduce | flops 384 | bytes 3072 | tf_op jit(solution)/shard_map/psum | solution.py:24
  32.5 2.3 fusion.8
  34.8 0.0 all-gather.12.cloned.1.call-start
  34.8 0.7 all-gather.12.cloned.1.call-update
  35.5 0.0 all-gather.10.cloned.1.call-start
  35.6 0.5 all-gather.10.cloned.1.call-update
  36.1 0.0 all-gather.14.cloned.1.call-start
  36.1 0.5 all-gather.14.cloned.1.call-update
  36.8 0.1 iota_compare_fusion.1
  36.9 0.1 broadcast_and_fusion
  37.0 0.0 all-gather.8.cloned.1.call-done
  37.0 93.9 %all-gather.6.cloned.1.call-done = bf16[384,8192]{1,0:T(8,128)(2,1)} async-done(((bf16[384,1024]{1,0:T(8,128)(2,1)}), bf16[384,8192]{1,0:T(8,128)(2,1)}) %all-gather.6.cloned.1.call-update) | async-done | bytes 6291472 | tf_op jit(solution)/shard_map/all_gather | solution.py:26
  130.9 5.1 %convolution_convert_fusion.3 = bf16[384,64]{0,1:T(8,128)(2,1)S(1)} fusion(bf16[384,8192]{1,0:T(8,128)(2,1)} %all-gather.6.cloned.1.call-done, bf16[8192,64]{0,1:T(8,128)(2,1)} %all-gather.8.cloned.1.call-done), kind=kOutput, calls=%fused_computation.24 | convolution fusion | flops 402677760 | bytes 7389184 | tf_op jit(solution)/shard_map/dot_general | solution.py:38
  136.0 31.0 %all_gather.23 = bf16[384,512]{0,1:T(8,128)(2,1)S(1)} all-gather(bf16[384,64]{0,1:T(8,128)(2,1)S(1)} %convolution_convert_fusion.3), channel_id=1, replica_groups=mesh['tp'=8,'rep'=4] {'tp'}, dimensions={1}, use_global_device_ids=true | all-gather | bytes 442368 | tf_op jit(solution)/shard_map/all_gather | solution.py:45
  167.0 0.3 reshape.108
  167.2 0.4 copy.14
  167.7 0.0 all-gather.12.cloned.1.call-done
  167.7 5.1 %convolution_convert_fusion.2 = bf16[384,64]{0,1:T(8,128)(2,1)S(1)} fusion(bf16[384,8192]{1,0:T(8,128)(2,1)} %all-gather.6.cloned.1.call-done, bf16[8192,64]{0,1:T(8,128)(2,1)} %all-gather.12.cloned.1.call-done), kind=kOutput, calls=%fused_computation.23 | convolution fusion | flops 402677760 | bytes 7389184 | tf_op jit(solution)/shard_map/dot_general | solution.py:38
  172.8 31.0 %all_gather.26 = bf16[384,512]{0,1:T(8,128)(2,1)S(1)} all-gather(bf16[384,64]{0,1:T(8,128)(2,1)S(1)} %convolution_convert_fusion.2), channel_id=1, replica_groups=mesh['tp'=8,'rep'=4] {'tp'}, dimensions={1}, use_global_device_ids=true | all-gather | bytes 442368 | tf_op jit(solution)/shard_map/all_gather | solution.py:44
  203.8 0.3 reshape.109
  204.1 0.4 copy.16
  204.5 0.6 gather_fusion
  205.1 0.6 gather_fusion.1
  205.8 0.1 select_bitcast_fusion.1
  205.9 1.2 all-gather.10.cloned.1.call-done
  207.1 8.6 %convolution_convert_fusion.1 = bf16[384,512]{1,0:T(8,128)(2,1)S(1)} fusion(bf16[384,8192]{1,0:T(8,128)(2,1)} %all-gather.6.cloned.1.call-done, bf16[8192,512]{1,0:T(8,128)(2,1)} %all-gather.10.cloned.1.call-done), kind=kOutput, calls=%fused_computation.21 | convolution fusion | flops 3221422080 | bytes 15073280 | tf_op jit(solution)/shard_map/dot_general | solution.py:38
  215.7 0.1 reshape.83
  215.8 0.7 fusion.31
  216.5 0.5 fusion.13
  217.0 0.3 copy.21
  217.3 0.1 copy.51
  217.4 1.5 collective-permute-start
  218.9 12.5 %collective-permute-done = bf16[384,512]{1,0:T(8,128)(2,1)S(1)} collective-permute-done((bf16[384,512]{1,0:T(8,128)(2,1)S(1)}, bf16[384,512]{1,0:T(8,128)(2,1)S(1)}, u32[]{:S(2)}, u32[]{:S(2)}) %collective-permute-start) | collective-permute-done | bytes 393248 | tf_op jit(solution)/shard_map/ppermute | solution.py:81
  231.4 13.1 %collective-permute-done.1 = bf16[384,512]{1,0:T(8,128)(2,1)S(1)} collective-permute-done((bf16[384,512]{1,0:T(8,128)(2,1)S(1)}, bf16[384,512]{1,0:T(8,128)(2,1)S(1)}, u32[]{:S(2)}, u32[]{:S(2)}) %collective-permute-start.1) | collective-permute-done | bytes 393248 | tf_op jit(solution)/shard_map/ppermute | solution.py:81
  244.5 12.3 %collective-permute-done.2 = bf16[384,512]{1,0:T(8,128)(2,1)S(1)} collective-permute-done((bf16[384,512]{1,0:T(8,128)(2,1)S(1)}, bf16[384,512]{1,0:T(8,128)(2,1)S(1)}, u32[]{:S(2)}, u32[]{:S(2)}) %collective-permute-start.2) | collective-permute-done | bytes 393248 | tf_op jit(solution)/shard_map/ppermute | solution.py:81
  256.8 11.4 %collective-permute-done.3 = bf16[384,512]{1,0:T(8,128)(2,1)S(1)} collective-permute-done((bf16[384,512]{1,0:T(8,128)(2,1)S(1)}, bf16[384,512]{1,0:T(8,128)(2,1)S(1)}, u32[]{:S(2)}, u32[]{:S(2)}) %collective-permute-start.3) | collective-permute-done | bytes 393248 | tf_op jit(solution)/shard_map/ppermute | solution.py:81
  268.2 10.5 %collective-permute-done.4 = bf16[384,512]{1,0:T(8,128)(2,1)S(1)} collective-permute-done((bf16[384,512]{1,0:T(8,128)(2,1)S(1)}, bf16[384,512]{1,0:T(8,128)(2,1)S(1)}, u32[]{:S(2)}, u32[]{:S(2)}) %collective-permute-start.4) | collective-permute-done | bytes 393248 | tf_op jit(solution)/shard_map/ppermute | solution.py:81
  278.7 10.6 %collective-permute-done.5 = bf16[384,512]{1,0:T(8,128)(2,1)} collective-permute-done((bf16[384,512]{1,0:T(8,128)(2,1)S(1)}, bf16[384,512]{1,0:T(8,128)(2,1)}, u32[]{:S(2)}, u32[]{:S(2)}) %collective-permute-start.5) | collective-permute-done | bytes 393248 | tf_op jit(solution)/shard_map/ppermute | solution.py:81
  289.3 0.1 lt.59
  289.4 10.7 %collective-permute-done.6 = bf16[384,512]{1,0:T(8,128)(2,1)} collective-permute-done((bf16[384,512]{1,0:T(8,128)(2,1)}, bf16[384,512]{1,0:T(8,128)(2,1)}, u32[]{:S(2)}, u32[]{:S(2)}) %collective-permute-start.6) | collective-permute-done | bytes 393248 | tf_op jit(solution)/shard_map/ppermute | solution.py:81
  300.1 1.8 constant_dynamic-update-slice_fusion.15
  301.9 1.8 constant_dynamic-update-slice_fusion.14
  303.7 0.8 constant_dynamic-update-slice_fusion.13
  304.5 0.8 constant_dynamic-update-slice_fusion.12
  305.3 0.9 constant_dynamic-update-slice_fusion.11
  306.1 0.9 constant_dynamic-update-slice_fusion.10
  307.0 0.9 constant_dynamic-update-slice_fusion.9
  307.9 0.9 constant_dynamic-update-slice_fusion.8
  308.7 1.8 constant_dynamic-update-slice_fusion.7
  310.5 1.8 constant_dynamic-update-slice_fusion.6
  312.4 0.8 constant_dynamic-update-slice_fusion.5
  313.2 0.8 constant_dynamic-update-slice_fusion.4
  314.0 0.8 constant_dynamic-update-slice_fusion.3
  314.8 0.8 constant_dynamic-update-slice_fusion.2
  315.6 0.8 constant_dynamic-update-slice_fusion.1
  316.4 0.8 constant_dynamic-update-slice_fusion
  317.2 7.9 %fusion.5 = (f32[384]{0:T(512)S(1)}, bf16[384,1024]{1,0:T(8,128)(2,1)S(1)}) fusion(bf16[4096,1024]{1,0:T(8,128)(2,1)} %all-gather.14.cloned.1.call-done, bf16[384,8192]{1,0:T(8,128)(2,1)} %constant_dynamic-update-slice_fusion, s32[]{:T(128)S(6)} %select_n.37, bf16[384,1024]{1,0:T(8,128)(2,1)S(1)} %copy-done.1), kind=kOutput, calls=%fused_computation.12 | convolution fusion | flops 3223584256 | bytes 13108740 | tf_op jit(solution)/shard_map/dot_general | solution.py:86
  325.1 1.5 fusion.4
  326.6 33.0 %all-reduce = (f32[384,6]{0,1:T(8,128)S(1)}, f32[384]{0:T(512)S(1)}) all-reduce(f32[384,6]{0,1:T(8,128)S(1)} %fusion.4, f32[384]{0:T(512)S(1)} %get-tuple-element.9), channel_id=1, replica_groups=mesh['tp'=8,'rep'=4] {'tp'}, use_global_device_ids=true, to_apply=%region_4.6 | all-reduce | flops 2688 | bytes 21504 | tf_op jit(solution)/shard_map/psum | solution.py:95
  359.6 0.6 multiply_select_fusion.1
  (24 shorter events, 0.1 us)
Async XLA Ops:
  7.2 317.9 %copy-start = (f32[1024,6]{0,1:T(8,128)S(1)}, f32[1024,6]{0,1:T(8,128)}, u32[]{:S(2)}) copy-start(f32[1024,6]{0,1:T(8,128)} %param.19) | copy-start | bytes 73732
  7.2 29.6 %copy-start.4 = (s32[2]{0:T(128)S(1)}, s32[2]{0:T(128)}, u32[]{:S(2)}) copy-start(s32[2]{0:T(128)} %param.12) | copy-start | bytes 28
  7.2 29.8 %all-gather.8.cloned.1.call-start = ((), (), s32[]{:S(2)}) async-start(), calls=%async_computation.1 | async-start | bytes 1310720 | tf_op jit(solution)/shard_map/all_gather | solution.py:34
  7.9 123.0 %all-gather.6.cloned.1.call-start = ((), (), s32[]{:S(2)}) async-start(), calls=%async_computation | async-start | bytes 7077888 | tf_op jit(solution)/shard_map/all_gather | solution.py:26
  34.8 132.9 %all-gather.12.cloned.1.call-start = ((), (), s32[]{:S(2)}) async-start(), calls=%async_computation.3 | async-start | bytes 1310720 | tf_op jit(solution)/shard_map/all_gather | solution.py:33
  35.5 171.6 %all-gather.10.cloned.1.call-start = ((), (), s32[]{:S(2)}) async-start(), calls=%async_computation.2 | async-start | bytes 10485760 | tf_op jit(solution)/shard_map/all_gather | solution.py:32
  36.1 281.1 %all-gather.14.cloned.1.call-start = ((), (), s32[]{:S(2)}) async-start(), calls=%async_computation.4 | async-start | bytes 10485760 | tf_op jit(solution)/shard_map/all_gather | solution.py:88
  217.4 14.0 %collective-permute-start = (bf16[384,512]{1,0:T(8,128)(2,1)S(1)}, bf16[384,512]{1,0:T(8,128)(2,1)S(1)}, u32[]{:S(2)}, u32[]{:S(2)}) collective-permute-start(bf16[384,512]{1,0:T(8,128)(2,1)S(1)} %bitcast.30), channel_id=1, source_target_pairs={{0,4},{4,8},{8,12},{12,16},{16,20},{20,24},{24,28},{28,0},{1,5},{5... | collective-permute-start | bytes 1179656 | tf_op jit(solution)/shard_map/ppermute | solution.py:81
  231.4 13.1 %collective-permute-start.1 = (bf16[384,512]{1,0:T(8,128)(2,1)S(1)}, bf16[384,512]{1,0:T(8,128)(2,1)S(1)}, u32[]{:S(2)}, u32[]{:S(2)}) collective-permute-start(bf16[384,512]{1,0:T(8,128)(2,1)S(1)} %collective-permute-done), channel_id=1, source_target_pairs={{0,4},{4,8},{8,12},{12,16},{16,20},{20,24},{24,28},{28,0},{1,5},{5... | collective-permute-start | bytes 1179656 | tf_op jit(solution)/shard_map/ppermute | solution.py:81
  244.5 12.3 %collective-permute-start.2 = (bf16[384,512]{1,0:T(8,128)(2,1)S(1)}, bf16[384,512]{1,0:T(8,128)(2,1)S(1)}, u32[]{:S(2)}, u32[]{:S(2)}) collective-permute-start(bf16[384,512]{1,0:T(8,128)(2,1)S(1)} %collective-permute-done.1), channel_id=1, source_target_pairs={{0,4},{4,8},{8,12},{12,16},{16,20},{20,24},{24,28},{28,0},{1,5},{5... | collective-permute-start | bytes 1179656 | tf_op jit(solution)/shard_map/ppermute | solution.py:81
  256.8 11.4 %collective-permute-start.3 = (bf16[384,512]{1,0:T(8,128)(2,1)S(1)}, bf16[384,512]{1,0:T(8,128)(2,1)S(1)}, u32[]{:S(2)}, u32[]{:S(2)}) collective-permute-start(bf16[384,512]{1,0:T(8,128)(2,1)S(1)} %collective-permute-done.2), channel_id=1, source_target_pairs={{0,4},{4,8},{8,12},{12,16},{16,20},{20,24},{24,28},{28,0},{1,5},{5... | collective-permute-start | bytes 1179656 | tf_op jit(solution)/shard_map/ppermute | solution.py:81
  268.2 10.5 %collective-permute-start.4 = (bf16[384,512]{1,0:T(8,128)(2,1)S(1)}, bf16[384,512]{1,0:T(8,128)(2,1)S(1)}, u32[]{:S(2)}, u32[]{:S(2)}) collective-permute-start(bf16[384,512]{1,0:T(8,128)(2,1)S(1)} %collective-permute-done.3), channel_id=1, source_target_pairs={{0,4},{4,8},{8,12},{12,16},{16,20},{20,24},{24,28},{28,0},{1,5},{5... | collective-permute-start | bytes 1179656 | tf_op jit(solution)/shard_map/ppermute | solution.py:81
  278.7 10.6 %collective-permute-start.5 = (bf16[384,512]{1,0:T(8,128)(2,1)S(1)}, bf16[384,512]{1,0:T(8,128)(2,1)}, u32[]{:S(2)}, u32[]{:S(2)}) collective-permute-start(bf16[384,512]{1,0:T(8,128)(2,1)S(1)} %collective-permute-done.4), channel_id=1, source_target_pairs={{0,4},{4,8},{8,12},{12,16},{16,20},{20,24},{24,28},{28,0},{1,5},{5... | collective-permute-start | bytes 1179656 | tf_op jit(solution)/shard_map/ppermute | solution.py:81
  289.3 10.8 %collective-permute-start.6 = (bf16[384,512]{1,0:T(8,128)(2,1)}, bf16[384,512]{1,0:T(8,128)(2,1)}, u32[]{:S(2)}, u32[]{:S(2)}) collective-permute-start(bf16[384,512]{1,0:T(8,128)(2,1)} %collective-permute-done.5), channel_id=1, source_target_pairs={{0,4},{4,8},{8,12},{12,16},{16,20},{20,24},{24,28},{28,0},{1,5},{5... | collective-permute-start | bytes 1179656 | tf_op jit(solution)/shard_map/ppermute | solution.py:81
  289.4 27.8 %copy-start.1 = (bf16[384,1024]{1,0:T(8,128)(2,1)S(1)}, bf16[384,1024]{1,0:T(8,128)(2,1)}, u32[]{:S(2)}) copy-start(bf16[384,1024]{1,0:T(8,128)(2,1)} %param.11) | copy-start | bytes 2359300
  317.2 7.9 %copy-start.3 = (f32[1024]{0:T(1024)S(1)}, f32[1024]{0:T(1024)}, u32[]{:S(2)}) copy-start(f32[1024]{0:T(1024)} %param.18) | copy-start | bytes 12292
  325.1 35.2 %copy-start.2 = (bf16[384,1024]{1,0:T(8,128)(2,1)}, bf16[384,1024]{1,0:T(8,128)(2,1)S(1)}, u32[]{:S(2)}) copy-start(bf16[384,1024]{1,0:T(8,128)(2,1)S(1)} %get-tuple-element.10) | copy-start | bytes 2359300
Sparse Core Ops, SparseCore 0:
  9.6 19.4 all-gather.7
  34.9 95.9 all-gather.5
  132.5 14.8 all-gather.11
  148.8 58.2 all-gather.9
  208.5 58.2 all-gather.13
